TPU v7x, 32 devices: a whole 2x2x4 slice. The times are simulated.
32 devices in a mesh: tm: 8 (over z, y), row: 2 (over core), col: 2 (over x).
Axes of the slice: x: 2, y: 2, z: 4, core: 2. Of those that a mesh axis runs over, the one named last changes fastest.
Arguments:
- precision_diag: float32 [16, 512, 512], P('tm', 'row', 'col'), may hold values from -4 to 16
- precision_link: float32 [16, 512, 512], P('tm', 'row', 'col'), may hold values from -8 to 2
Outputs:
- pivots: float32 [16, 512, 512], P('tm', 'row', 'col')
- couplings: float32 [16, 512, 512], P('tm', 'row', 'col')
- log_variance: float32 [16, 512], P('tm', ('row', 'col'))
All inputs are finite; a program needn't handle non-finite values.
Results may differ from a plain program's by a relative error of at most 0.0003.
Values sent between devices are 32-bit elements; how exact they have to be, the bound alone decides.
A program may use at most 128 MiB of HBM per device.

v0:
```python
import jax
import jax.numpy as jnp
from jax import lax
from jax.sharding import PartitionSpec as P

LEVELS = 4


def shifted(array, axis, by):
    devices = lax.axis_size(axis)
    pairs = [(i, i + by) for i in range(devices) if 0 <= i + by < devices]
    return lax.ppermute(array, axis, pairs)


def product_tn(left_part, right_part):
    return jnp.einsum("ki,kl->il", left_part, right_part, precision=lax.Precision.HIGHEST)


def factor_solve(pivot, right_side):
    lower_factor = jnp.linalg.cholesky(pivot)
    return jax.scipy.linalg.solve_triangular(lower_factor, right_side, lower=True)


def unit_columns(node_count, diag_id):
    quarter = node_count // 4
    row_positions = jnp.arange(node_count)[:, None]
    col_positions = diag_id * quarter + jnp.arange(quarter)[None, :]
    return (row_positions == col_positions).astype(jnp.float32)


def log_variance(inverse_cols):
    return jnp.log(jnp.sum(inverse_cols * inverse_cols, axis=0))


def column_half(panel, index_id):
    half_width = panel.shape[1] // 2
    return lax.dynamic_slice_in_dim(panel, index_id * half_width, half_width, 1)


def whole_blocks(stacked):
    widened = lax.all_gather(stacked, "col", axis=2, tiled=True)
    return lax.all_gather(widened, "row", axis=1, tiled=True)


def send_later(gram_up, link_new, stride):
    return shifted((gram_up, link_new), "tm", stride)


def guarded(active, compute, zero_fill, operands):
    if active is None:
        return compute(operands)
    return lax.cond(active, compute, zero_fill, operands)


def solve_divided(operands, place):
    row_id, col_id, diag_id = place
    pivot, below_cols, above_rows = operands
    node_count = pivot.shape[0]
    half_width = below_cols.shape[1]
    right_side = jnp.concatenate(
        [below_cols, above_rows.T, unit_columns(node_count, diag_id)], axis=1
    )
    solved = factor_solve(pivot, right_side)
    lower_own = solved[:, :half_width]
    upper_own = solved[:, half_width : 2 * half_width]
    log_part = log_variance(solved[:, 2 * half_width :])
    return (log_part, lower_own, upper_own, -product_tn(upper_own, lower_own))


def gram_divided(panels, place):
    row_id, col_id, diag_id = place
    lower_whole, upper_whole = panels
    return (
        product_tn(column_half(lower_whole, row_id), column_half(lower_whole, col_id)),
        product_tn(column_half(upper_whole, row_id), column_half(upper_whole, col_id)),
    )


def eliminate(pivot_tile, below_tile, above_tile, active, place):
    half_width = pivot_tile.shape[0]
    node_count = 2 * half_width
    log_zero = jnp.zeros((node_count // 4,), jnp.float32)
    tile_zero = jnp.zeros((half_width, half_width), jnp.float32)
    pivot = whole_blocks(pivot_tile[None])[0]
    below_cols = lax.all_gather(below_tile, "row", axis=0, tiled=True)
    above_rows = lax.all_gather(above_tile, "col", axis=1, tiled=True)
    panel_zero = jnp.zeros((node_count, half_width), jnp.float32)
    log_part, lower_own, upper_own, link_new = guarded(
        active,
        lambda operands: solve_divided(operands, place),
        lambda operands: (log_zero, panel_zero, panel_zero, tile_zero),
        (pivot, below_cols, above_rows),
    )
    lower_whole = lax.all_gather(lower_own, "col", axis=1, tiled=True)
    upper_whole = lax.all_gather(upper_own, "row", axis=1, tiled=True)
    gram_down, gram_up = guarded(
        active,
        lambda operands: gram_divided(operands, place),
        lambda operands: (tile_zero, tile_zero),
        (lower_whole, upper_whole),
    )
    return (log_part, gram_down, gram_up, link_new)


def final_log(pivot, place):
    row_id, col_id, diag_id = place
    inverse_cols = factor_solve(pivot, unit_columns(pivot.shape[0], diag_id))
    return log_variance(inverse_cols)


def shards(precision_diag, precision_link):
    row_id = lax.axis_index("row")
    col_id = lax.axis_index("col")
    time_id = lax.axis_index("tm")
    place = (row_id, col_id, row_id * 2 + col_id)
    device_count = lax.axis_size("tm")
    pivot_low = precision_diag[0]
    pivot_high = precision_diag[1]
    link_low = precision_link[0]
    link_high = jnp.where(
        time_id == device_count - 1, jnp.zeros_like(precision_link[1]), precision_link[1]
    )
    log_high, gram_down, gram_up, link_low = eliminate(pivot_high, link_low, link_high, None, place)
    ahead_gram, from_below = send_later(gram_up, link_low, 1)
    pivot_low = pivot_low - gram_down - ahead_gram
    log_low = jnp.zeros_like(log_high)
    for level_num in range(1, LEVELS):
        stride = 2 ** (level_num - 1)
        position = time_id % (2 * stride)
        active = position == stride
        keeper = position == 0
        below_link = from_below
        log_now, gram_down, gram_up, link_new = eliminate(
            pivot_low, below_link, link_low, active, place
        )
        back_gram, back_link = shifted((gram_down, link_new), "tm", -stride)
        ahead_gram, from_below = send_later(gram_up, link_new, stride)
        log_low = jnp.where(active, log_now, log_low)
        pivot_low = pivot_low - back_gram - ahead_gram
        link_low = jnp.where(keeper, back_link, link_low)
    remaining = time_id % 2 ** (LEVELS - 1) == 0
    whole_pivot = whole_blocks(pivot_low[None])[0]
    log_final = lax.cond(
        remaining,
        lambda pivot: final_log(pivot, place),
        lambda pivot: jnp.zeros_like(log_low),
        whole_pivot,
    )
    log_low = jnp.where(remaining, log_final, log_low)
    pivots = jnp.stack([pivot_low, pivot_high])
    couplings = jnp.stack([link_low, link_high])
    logs = jnp.stack([log_low, log_high])
    return (pivots, couplings, logs)


def solution(mesh):
    in_specs = (P("tm", "row", "col"), P("tm", "row", "col"))
    out_specs = (P("tm", "row", "col"), P("tm", "row", "col"), P("tm", ("row", "col")))
    return jax.shard_map(shards, mesh=mesh, in_specs=in_specs, out_specs=out_specs, check_vma=False)
```

profile of v0, /device:TPU:0, one launch (start us, length us, event | category | flops | bytes accessed | tf_op | source)
XLA Modules:
  0.0 1136.3 jit_solution(9765226666093898980)
XLA Ops:
  9.2 10.0 all_gather.78
  21.7 9.0 all-gather.1
  31.0 2.6 copy.11
  36.1 11.7 %cholesky.838 = f32[128,128]{1,0:T(8,128)S(1)} custom-call(f32[128,128]{1,0:T(8,128)S(1)} %cholesky.958), custom_call_target="Cholesky" | custom-call | tf_op jit(solution)/shard_map/jit(cholesky)/cholesky | solution.py:20
  47.8 9.8 custom-call.57
  60.3 11.7 %cholesky.857 = f32[128,128]{1,0:T(8,128)S(1)} custom-call(f32[128,128]{1,0:T(8,128)S(1)} %cholesky.962), custom_call_target="Cholesky" | custom-call | tf_op jit(solution)/shard_map/jit(cholesky)/cholesky | solution.py:20
  72.1 10.1 custom-call.58
  83.8 11.7 %cholesky.878 = f32[128,128]{1,0:T(8,128)S(1)} custom-call(f32[128,128]{1,0:T(8,128)S(1)} %cholesky.967), custom_call_target="Cholesky" | custom-call | tf_op jit(solution)/shard_map/jit(cholesky)/cholesky | solution.py:20
  96.2 9.8 custom-call.59
  107.5 11.7 %cholesky.895 = f32[128,128]{1,0:T(8,128)S(1)} custom-call(f32[128,128]{1,0:T(8,128)S(1)} %convolution_subtract_fusion.30), custom_call_target="Cholesky" | custom-call | tf_op jit(solution)/shard_map/jit(cholesky)/cholesky | solution.py:20
  124.5 11.6 %while.13 = (s32[]{:T(128)}, f32[512,512]{1,0:T(8,128)}, s32[4,2]{0,1:T(2,128)S(1)}, f32[4,128,128]{2,1,0:T(8,128)S(1)}, s32[]{:T(128)}) while((s32[]{:T(128)}, f32[512,512]{1,0:T(8,128)}, s32[4,2]{0,1:T(2,128)S(1)}, f32[4,128,128]{2,1,0:T(8,128)S(1)}, s32[]{:T(128)}) %tuple.211), condition=%wide.while_cond.clone.2, body=%wide.while_body.clone.2.sunk | while | flops 2 | bytes 131189 | solution.py:21
  125.1 2.3 bitcast_dynamic-update-slice_fusion.10
  128.0 2.3 bitcast_dynamic-update-slice_fusion.10
  131.0 2.3 bitcast_dynamic-update-slice_fusion.10
  133.9 2.2 bitcast_dynamic-update-slice_fusion.10
  136.1 39.3 %custom-call.60 = f32[4,128,128]{1,2,0:T(8,128)S(1)} custom-call(f32[4,128,128]{2,1,0:T(8,128)S(1)} %get-tuple-element.163), custom_call_target="InvertDiagBlocksLowerTriangular" | custom-call | tf_op jit(solution)/shard_map/jit(_solve_triangular)/triangular_solve | solution.py:21
  180.6 2.8 convolution_subtract_fusion.26
  185.9 9.9 all-gather.28.cloned.1.call-done
  195.8 2.3 fusion.162
  198.1 3.7 collective-permute-start
  201.9 18.5 %all-gather.26.cloned.1.call-done = f32[512,512]{1,0:T(8,128)} async-done(((f32[512,256]{1,0:T(8,128)}), f32[512,512]{1,0:T(8,128)}) %all-gather.26.cloned.1.call-update) | async-done | bytes 1048592 | tf_op jit(solution)/shard_map/all_gather | solution.py:94
  220.4 2.3 fusion.152
  222.7 8.6 all-gather.2
  232.4 3.4 collective-permute-start.1
  235.8 7.3 all_gather.86
  245.3 5.0 conditional.7
  251.0 184.8 %all-gather.30.cloned.1.call-done = f32[512,512]{1,0:T(8,128)} async-done(((f32[512,256]{1,0:T(8,128)}), f32[512,512]{1,0:T(8,128)}) %all-gather.30.cloned.1.call-update) | async-done | bytes 1048592 | tf_op jit(solution)/shard_map/all_gather | solution.py:94
  435.8 11.0 all-gather.32.cloned.1.call-done
  447.2 7.1 collective-permute-start.3
  455.6 10.3 collective-permute-done.3
  466.0 8.4 all-gather.4
  476.0 5.0 collective-permute-start.5
  481.0 3.0 collective-permute-done.4
  484.0 7.0 all_gather.92
  491.1 2.3 all_gather.93
  493.4 4.8 conditional.9
  499.0 192.1 %all-gather.34.cloned.1.call-done = f32[512,512]{1,0:T(8,128)} async-done(((f32[512,256]{1,0:T(8,128)}), f32[512,512]{1,0:T(8,128)}) %all-gather.34.cloned.1.call-update) | async-done | bytes 1048592 | tf_op jit(solution)/shard_map/all_gather | solution.py:94
  691.1 11.2 all-gather.36.cloned.1.call-done
  702.6 7.1 collective-permute-start.7
  711.0 4.7 collective-permute-done.7
  715.7 4.1 collective-permute-done.6
  720.6 8.1 all-gather.6
  730.3 4.6 collective-permute-start.9
  734.9 2.4 collective-permute-done.8
  737.4 7.0 all_gather.98
  744.4 2.3 all_gather.99
  746.7 5.0 conditional.11
  752.4 184.5 %all-gather.38.cloned.1.call-done = f32[512,512]{1,0:T(8,128)} async-done(((f32[512,256]{1,0:T(8,128)}), f32[512,512]{1,0:T(8,128)}) %all-gather.38.cloned.1.call-update) | async-done | bytes 1048592 | tf_op jit(solution)/shard_map/all_gather | solution.py:94
  936.9 11.0 all-gather.40.cloned.1.call-done
  948.3 8.0 collective-permute-start.11
  957.6 4.8 collective-permute-done.11
  962.4 8.2 collective-permute-done.10
  970.7 9.1 all-gather.8
  981.4 8.7 collective-permute-done.12
  992.0 136.6 %conditional.13 = (f32[128]{0:T(128)S(1)}) conditional(s32[]{:T(128)} %convert_element_type.34, () %tuple.76, (f32[1,512,512]{1,2,0:T(8,128)}, s32[]{:T(128)}) %tuple.257), branch_computations={%region_23.26_spmd, %region_24.28_spmd} | conditional | flops 656916992 | bytes 27548512 | solution.py:143
  995.2 11.7 %cholesky.766 = f32[128,128]{1,0:T(8,128)S(1)} custom-call(f32[128,128]{1,0:T(8,128)S(1)} %cholesky.919), custom_call_target="Cholesky" | custom-call | tf_op jit(solution)/shard_map/cond/branch_1_fun/jit(cholesky)/cholesky | solution.py:20
  1006.9 9.8 custom-call.54
  1017.6 11.7 %cholesky.785 = f32[128,128]{1,0:T(8,128)S(1)} custom-call(f32[128,128]{1,0:T(8,128)S(1)} %cholesky.923), custom_call_target="Cholesky" | custom-call | tf_op jit(solution)/shard_map/cond/branch_1_fun/jit(cholesky)/cholesky | solution.py:20
  1031.3 10.0 custom-call.55
  1042.0 11.7 %cholesky.806 = f32[128,128]{1,0:T(8,128)S(1)} custom-call(f32[128,128]{1,0:T(8,128)S(1)} %cholesky.928), custom_call_target="Cholesky" | custom-call | tf_op jit(solution)/shard_map/cond/branch_1_fun/jit(cholesky)/cholesky | solution.py:20
  1055.0 9.8 custom-call.56
  1065.4 11.7 %cholesky.823 = f32[128,128]{1,0:T(8,128)S(1)} custom-call(f32[128,128]{1,0:T(8,128)S(1)} %convolution_subtract_fusion.11), custom_call_target="Cholesky" | custom-call | tf_op jit(solution)/shard_map/cond/branch_1_fun/jit(cholesky)/cholesky | solution.py:20
  1078.9 8.1 while.12
  1087.0 39.3 %custom-call.26 = f32[4,128,128]{1,2,0:T(8,128)S(1)} custom-call(f32[4,128,128]{2,1,0:T(8,128)S(1)} %get-tuple-element.141), custom_call_target="InvertDiagBlocksLowerTriangular" | custom-call | tf_op jit(solution)/shard_map/cond/branch_1_fun/jit(_solve_triangular)/triangular_solve | solution.py:21
  (237 shorter events, 66.7 us)
Async XLA Ops:
  7.2 12.1 %copy-start.38 = (f32[2,256,256]{2,1,0:T(8,128)S(1)}, f32[2,256,256]{2,1,0:T(8,128)}, u32[]{:S(2)}) copy-start(f32[2,256,256]{2,1,0:T(8,128)} %param.20) | copy-start | bytes 1572868
  7.2 23.8 %all-gather.24.cloned.1.call-start = ((), (), s32[]{:S(2)}) async-start(), calls=%async_computation | async-start | bytes 1572864 | tf_op jit(solution)/shard_map/all_gather | solution.py:42
  9.2 10.3 copy-start.17
  19.2 176.6 %all-gather.28.cloned.1.call-start = ((), (), s32[]{:S(2)}) async-start(), calls=%async_computation.2 | async-start | bytes 1572864 | tf_op jit(solution)/shard_map/all_gather | solution.py:95
  19.4 11.6 %copy-start.19 = (f32[1,256,256]{2,1,0:T(8,128)}, f32[1,256,256]{2,1,0:T(8,128)S(1)}, u32[]{:S(2)}) copy-start(f32[1,256,256]{2,1,0:T(8,128)S(1)} %get-tuple-element.290) | copy-start | bytes 786436
  31.0 2.6 copy-start.6
  35.1 1.0 copy-start.12
  180.6 3.4 copy-start
  185.1 16.7 %copy-start.37 = (f32[1,256,256]{2,1,0:T(8,128)S(1)}, f32[1,256,256]{2,1,0:T(8,128)}, u32[]{:S(2)}) copy-start(f32[1,256,256]{2,1,0:T(8,128)} %get-tuple-element.287) | copy-start | bytes 786436
  185.1 35.3 %all-gather.26.cloned.1.call-start = ((), (), s32[]{:S(2)}) async-start(), calls=%async_computation.1 | async-start | bytes 1572864 | tf_op jit(solution)/shard_map/all_gather | solution.py:94
  185.8 59.5 %all-gather.42.cloned.1.call-start = ((), (), s32[]{:S(2)}) async-start(), calls=%async_computation.9 | async-start | bytes 1572864 | tf_op jit(solution)/shard_map/all_gather | solution.py:42
  198.1 22.3 %collective-permute-start = (f32[256,256]{0,1:T(8,128)S(1)}, f32[256,256]{0,1:T(8,128)S(1)}, u32[]{:S(2)}, u32[]{:S(2)}) collective-permute-start(f32[256,256]{0,1:T(8,128)S(1)} %fusion.162), channel_id=1, source_target_pairs={{0,4},{4,8},{8,12},{12,16},{16,20},{20,24},{24,28},{1,5},{5,9},{9,... | collective-permute-start | bytes 786440 | tf_op jit(solution)/shard_map/ppermute | solution.py:12
  222.7 8.6 copy-start.15
  231.3 204.5 %all-gather.30.cloned.1.call-start = ((), (), s32[]{:S(2)}) async-start(), calls=%async_computation.3 | async-start | bytes 1572864 | tf_op jit(solution)/shard_map/all_gather | solution.py:94
  232.4 12.9 %copy-start.13 = (f32[256,256]{1,0:T(8,128)}, f32[256,256]{1,0:T(8,128)S(1)}, u32[]{:S(2)}) copy-start(f32[256,256]{1,0:T(8,128)S(1)} %convolution_negate_fusion.3) | copy-start | bytes 786436
  232.4 10.7 collective-permute-start.1
  250.4 196.5 %all-gather.32.cloned.1.call-start = ((), (), s32[]{:S(2)}) async-start(), calls=%async_computation.4 | async-start | bytes 1572864 | tf_op jit(solution)/shard_map/all_gather | solution.py:95
  250.9 242.4 %all-gather.44.cloned.1.call-start = ((), (), s32[]{:S(2)}) async-start(), calls=%async_computation.10 | async-start | bytes 1572864 | tf_op jit(solution)/shard_map/all_gather | solution.py:42
  446.9 19.1 %copy-start.16 = (f32[256,256]{0,1:T(8,128)S(1)}, f32[256,256]{0,1:T(8,128)}, u32[]{:S(2)}) copy-start(f32[256,256]{0,1:T(8,128)} %copy-done.15) | copy-start | bytes 786436
  447.2 36.8 %copy-start.14 = (f32[256,256]{1,0:T(8,128)S(1)}, f32[256,256]{1,0:T(8,128)}, u32[]{:S(2)}) copy-start(f32[256,256]{1,0:T(8,128)} %copy-done.13) | copy-start | bytes 786436
  447.2 18.7 %collective-permute-start.3 = (f32[256,256]{0,1:T(8,128)S(1)}, f32[256,256]{0,1:T(8,128)S(1)}, u32[]{:S(2)}, u32[]{:S(2)}) collective-permute-start(f32[256,256]{0,1:T(8,128)S(1)} %copy.17), channel_id=1, source_target_pairs={{0,4},{4,8},{8,12},{12,16},{16,20},{20,24},{24,28},{1,5},{5,9},{9,... | collective-permute-start | bytes 786440 | tf_op jit(solution)/shard_map/ppermute | solution.py:12
  454.3 11.6 %collective-permute-start.2 = (f32[256,256]{0,1:T(8,128)S(1)}, f32[256,256]{0,1:T(8,128)S(1)}, u32[]{:S(2)}, u32[]{:S(2)}) collective-permute-start(f32[256,256]{0,1:T(8,128)S(1)} %copy.16), channel_id=1, source_target_pairs={{4,0},{8,4},{12,8},{16,12},{20,16},{24,20},{28,24},{5,1},{9,5},{13... | collective-permute-start | bytes 786440 | tf_op jit(solution)/shard_map/ppermute | solution.py:12
  466.0 18.0 %copy-start.25 = (f32[256,256]{0,1:T(8,128)}, f32[256,256]{0,1:T(8,128)S(1)}, u32[]{:S(2)}) copy-start(f32[256,256]{0,1:T(8,128)S(1)} %subtract_subtract_fusion.2) | copy-start | bytes 786436
  474.5 216.6 %all-gather.34.cloned.1.call-start = ((), (), s32[]{:S(2)}) async-start(), calls=%async_computation.5 | async-start | bytes 1572864 | tf_op jit(solution)/shard_map/all_gather | solution.py:94
  474.5 9.4 collective-permute-start.4
  476.0 15.1 %collective-permute-start.5 = (f32[256,256]{0,1:T(8,128)S(1)}, f32[256,256]{0,1:T(8,128)S(1)}, u32[]{:S(2)}, u32[]{:S(2)}) collective-permute-start(f32[256,256]{0,1:T(8,128)S(1)} %copy.18), channel_id=1, source_target_pairs={{0,4},{4,8},{8,12},{12,16},{16,20},{20,24},{24,28},{1,5},{5,9},{9,... | collective-permute-start | bytes 786440 | tf_op jit(solution)/shard_map/ppermute | solution.py:12
  484.0 9.4 copy-start.23
  498.2 204.1 %copy-start.35 = (f32[256,256]{1,0:T(8,128)}, f32[256,256]{1,0:T(8,128)S(1)}, u32[]{:S(2)}) copy-start(f32[256,256]{1,0:T(8,128)S(1)} %get-tuple-element.117) | copy-start | bytes 786436
  498.3 204.0 %all-gather.36.cloned.1.call-start = ((), (), s32[]{:S(2)}) async-start(), calls=%async_computation.6 | async-start | bytes 1572864 | tf_op jit(solution)/shard_map/all_gather | solution.py:95
  499.0 247.7 %all-gather.46.cloned.1.call-start = ((), (), s32[]{:S(2)}) async-start(), calls=%async_computation.11 | async-start | bytes 1572864 | tf_op jit(solution)/shard_map/all_gather | solution.py:42
  702.3 17.6 %copy-start.26 = (f32[256,256]{0,1:T(8,128)S(1)}, f32[256,256]{0,1:T(8,128)}, u32[]{:S(2)}) copy-start(f32[256,256]{0,1:T(8,128)} %copy-done.25) | copy-start | bytes 786436
  702.6 26.2 %copy-start.36 = (f32[256,256]{1,0:T(8,128)S(1)}, f32[256,256]{1,0:T(8,128)}, u32[]{:S(2)}) copy-start(f32[256,256]{1,0:T(8,128)} %copy-done.35) | copy-start | bytes 786436
  702.6 34.7 %copy-start.24 = (f32[256,256]{1,0:T(8,128)S(1)}, f32[256,256]{1,0:T(8,128)}, u32[]{:S(2)}) copy-start(f32[256,256]{1,0:T(8,128)} %copy-done.23) | copy-start | bytes 786436
  702.6 13.1 %collective-permute-start.7 = (f32[256,256]{0,1:T(8,128)S(1)}, f32[256,256]{0,1:T(8,128)S(1)}, u32[]{:S(2)}, u32[]{:S(2)}) collective-permute-start(f32[256,256]{0,1:T(8,128)S(1)} %copy.20), channel_id=1, source_target_pairs={{0,8},{4,12},{8,16},{12,20},{16,24},{20,28},{1,9},{5,13},{9,17},{1... | collective-permute-start | bytes 786440 | tf_op jit(solution)/shard_map/ppermute | solution.py:12
  709.7 10.1 collective-permute-start.6
  719.9 0.7 copy-start.21
  728.8 208.1 %all-gather.38.cloned.1.call-start = ((), (), s32[]{:S(2)}) async-start(), calls=%async_computation.7 | async-start | bytes 1572864 | tf_op jit(solution)/shard_map/all_gather | solution.py:94
  728.9 8.5 collective-permute-start.8
  730.3 14.1 %collective-permute-start.9 = (f32[256,256]{0,1:T(8,128)S(1)}, f32[256,256]{0,1:T(8,128)S(1)}, u32[]{:S(2)}, u32[]{:S(2)}) collective-permute-start(f32[256,256]{0,1:T(8,128)S(1)} %copy.21), channel_id=1, source_target_pairs={{0,8},{4,12},{8,16},{12,20},{16,24},{20,28},{1,9},{5,13},{9,17},{1... | collective-permute-start | bytes 786440 | tf_op jit(solution)/shard_map/ppermute | solution.py:12
  737.4 9.4 copy-start.27
  751.7 196.2 %copy-start.39 = (f32[256,256]{1,0:T(8,128)}, f32[256,256]{1,0:T(8,128)S(1)}, u32[]{:S(2)}) copy-start(f32[256,256]{1,0:T(8,128)S(1)} %get-tuple-element.122) | copy-start | bytes 786436
  751.7 196.2 %all-gather.40.cloned.1.call-start = ((), (), s32[]{:S(2)}) async-start(), calls=%async_computation.8 | async-start | bytes 1572864 | tf_op jit(solution)/shard_map/all_gather | solution.py:95
  752.3 239.7 %all-gather.48.cloned.1.call-start = ((), (), s32[]{:S(2)}) async-start(), calls=%async_computation.12 | async-start | bytes 1572864 | tf_op jit(solution)/shard_map/all_gather | solution.py:42
  947.9 22.6 %copy-start.22 = (f32[256,256]{0,1:T(8,128)S(1)}, f32[256,256]{0,1:T(8,128)}, u32[]{:S(2)}) copy-start(f32[256,256]{0,1:T(8,128)} %copy-done.21) | copy-start | bytes 786436
  948.3 31.5 %copy-start.40 = (f32[256,256]{1,0:T(8,128)S(1)}, f32[256,256]{1,0:T(8,128)}, u32[]{:S(2)}) copy-start(f32[256,256]{1,0:T(8,128)} %copy-done.39) | copy-start | bytes 786436
  948.3 33.0 %copy-start.1 = (f32[128,640]{1,0:T(8,128)S(1)}, f32[128,640]{1,0:T(8,128)}, u32[]{:S(2)}) copy-start(f32[128,640]{1,0:T(8,128)} %copy-done) | copy-start | bytes 983044
  948.3 14.1 %collective-permute-start.11 = (f32[256,256]{0,1:T(8,128)S(1)}, f32[256,256]{0,1:T(8,128)S(1)}, u32[]{:S(2)}, u32[]{:S(2)}) collective-permute-start(f32[256,256]{0,1:T(8,128)S(1)} %copy.23), channel_id=1, source_target_pairs={{0,16},{4,20},{8,24},{12,28},{1,17},{5,21},{9,25},{13,29},{2,18},{... | collective-permute-start | bytes 786440 | tf_op jit(solution)/shard_map/ppermute | solution.py:12
  956.3 14.3 %collective-permute-start.10 = (f32[256,256]{0,1:T(8,128)S(1)}, f32[256,256]{0,1:T(8,128)S(1)}, u32[]{:S(2)}, u32[]{:S(2)}) collective-permute-start(f32[256,256]{0,1:T(8,128)S(1)} %copy.22), channel_id=1, source_target_pairs={{16,0},{20,4},{24,8},{28,12},{17,1},{21,5},{25,9},{29,13},{18,2},{... | collective-permute-start | bytes 786440 | tf_op jit(solution)/shard_map/ppermute | solution.py:12
  970.6 19.5 %copy-start.28 = (f32[256,256]{1,0:T(8,128)S(1)}, f32[256,256]{1,0:T(8,128)}, u32[]{:S(2)}) copy-start(f32[256,256]{1,0:T(8,128)} %copy-done.27) | copy-start | bytes 786436
  979.8 10.4 copy-start.20
  979.8 10.3 collective-permute-start.12
  981.3 9.7 copy-start.18
  992.2 1.8 copy-start.5
  994.2 1.0 copy-start.10
  995.2 21.7 %copy-start.11 = (f32[512,512]{1,0:T(8,128)S(1)}, f32[512,512]{1,0:T(8,128)}, u32[]{:S(2)}) copy-start(f32[512,512]{1,0:T(8,128)} %copy-done.10) | copy-start | bytes 3145732 | tf_op jit(solution)/shard_map/cond
Sparse Core Ops, SparseCore 0:
  19.4 10.5 all-gather.23
  185.2 10.5 all-gather.27
  197.9 22.4 all-gather.25
  231.4 9.0 all-gather.41
  250.5 185.3 all-gather.29
  437.8 9.0 all-gather.31
  474.6 10.2 all-gather.43
  498.4 192.6 all-gather.33
  693.2 9.0 all-gather.35
  728.9 8.0 all-gather.45
  751.9 184.9 all-gather.37
  938.9 9.0 all-gather.39
  979.9 6.2 all-gather.47
where the time goes:
time: 1150 us; the launch traced here: 1140 us
  waiting for transfers between devices  672 us (58%)
  other arithmetic  242 us (21%)
  blocking collectives  83.7 us (7%)
  starting transfers between devices  47.2 us (4%)
  local copies, waits for them, and re-layouts  37.3 us (3%)
  matrix products  23.3 us (2%)
  between operations  18.1 us (2%)
  loops' own time  13.3 us (1%)
    all_gather x4, waiting for transfers between devices, eliminate(): lower_whole = lax.all_gather(lower_own, 'col', axis=1, tiled=True)  580 us
    another operation x28, other arithmetic, factor_solve(): lower_factor = jnp.linalg.cholesky(pivot)  157 us
    another operation x8, other arithmetic, factor_solve(): jax.scipy.linalg.solve_triangular(lower_factor, right_side, lower=True)  80.2 us
    ppermute x13, starting transfers between devices, shifted(): return lax.ppermute(array, axis, pairs)  46.7 us
    ppermute x13, waiting for transfers between devices, shifted(): return lax.ppermute(array, axis, pairs)  46.3 us
    all_gather x5, blocking collectives, whole_blocks(): widened = lax.all_gather(stacked, 'col', axis=2, tiled=True)  44.3 us
    all_gather x4, waiting for transfers between devices, eliminate(): upper_whole = lax.all_gather(upper_own, 'row', axis=1, tiled=True)  43.2 us
    all_gather x4, blocking collectives, eliminate(): above_rows = lax.all_gather(above_tile, 'col', axis=1, tiled=True)  30.4 us
  transfers between devices with their start and end apart: 26, of which 16 were waited for; matrix products, arithmetic and copies ran while one was open for 1% of the time, Pallas kernels for 0%

commit v1 on v0

--- a/solution.py
+++ b/solution.py
@@ -91,7 +91,9 @@
         lambda operands: (log_zero, panel_zero, panel_zero, tile_zero),
         (pivot, below_cols, above_rows),
     )
-    lower_whole = lax.all_gather(lower_own, "col", axis=1, tiled=True)
+    lower_whole = jnp.concatenate(
+        lax.all_to_all(jnp.stack([lower_own] * lax.axis_size("col")), "col", 0, 0), axis=1
+    )
     upper_whole = lax.all_gather(upper_own, "row", axis=1, tiled=True)
     gram_down, gram_up = guarded(
         active,

time: 1150 us -> 1090 us (0.948)
  waiting for transfers between devices: 672 us -> 557 us
  starting transfers between devices: 47.2 us -> 96.9 us
    all_gather x4 -> x0, waiting for transfers between devices: 580 us -> none  [eliminate(): lower_whole = lax.all_gather(lower_own, 'col', axis=1, tiled=True)]
    all_gather x4, waiting for transfers between devices: 43.2 us -> 468 us  [eliminate(): upper_whole = lax.all_gather(upper_own, 'row', axis=1, tiled=True)]
    all_to_all x0 -> x4, waiting for transfers between devices: none -> 42.3 us  [eliminate(): lax.all_to_all(jnp.stack([lower_own] * lax.axis_size('col')), 'col', 0, 0)]
    ppermute x13, starting transfers between devices: 46.7 us -> 82.2 us  [shifted(): return lax.ppermute(array, axis, pairs)]
    all_to_all x0 -> x4, starting transfers between devices: none -> 14.3 us  [eliminate(): lax.all_to_all(jnp.stack([lower_own] * lax.axis_size('col')), 'col', 0, 0)]
  transfers between devices with their start and end apart: 26 -> 26, of which waited for: 16 -> 16; matrix products, arithmetic and copies ran while one was open for 1% -> 2% of each run, Pallas kernels for 0% -> 0%
where the time goes in v1:
time: 1090 us; the launch traced here: 1080 us
  waiting for transfers between devices  557 us (51%)
  other arithmetic  249 us (23%)
  starting transfers between devices  96.9 us (9%)
  blocking collectives  79.6 us (7%)
  local copies, waits for them, and re-layouts  40.8 us (4%)
  matrix products  21.7 us (2%)
  between operations  17.8 us (2%)
  loops' own time  13.7 us (1%)
    all_gather x4, waiting for transfers between devices, eliminate(): upper_whole = lax.all_gather(upper_own, 'row', axis=1, tiled=True)  468 us
    another operation x28, other arithmetic, factor_solve(): lower_factor = jnp.linalg.cholesky(pivot)  157 us
    ppermute x13, starting transfers between devices, shifted(): return lax.ppermute(array, axis, pairs)  82.2 us
    another operation x8, other arithmetic, factor_solve(): jax.scipy.linalg.solve_triangular(lower_factor, right_side, lower=True)  80.2 us
    ppermute x13, waiting for transfers between devices, shifted(): return lax.ppermute(array, axis, pairs)  46.4 us
    all_to_all x4, waiting for transfers between devices, eliminate(): lax.all_to_all(jnp.stack([lower_own] * lax.axis_size('col')), 'col', 0, 0)  42.3 us
    all_gather x5, blocking collectives, whole_blocks(): widened = lax.all_gather(stacked, 'col', axis=2, tiled=True)  40.2 us
    all_gather x4, blocking collectives, eliminate(): above_rows = lax.all_gather(above_tile, 'col', axis=1, tiled=True)  30.4 us
  transfers between devices with their start and end apart: 26, of which 16 were waited for; matrix products, arithmetic and copies ran while one was open for 2% of the time, Pallas kernels for 0%

profile of v1, /device:TPU:0, one launch (start us, length us, event | category | flops | bytes accessed | tf_op | source)
XLA Modules:
  0.0 1075.9 jit_solution(9866799419962216669)
XLA Ops:
  9.2 10.0 all_gather.66
  21.8 9.0 all-gather.1
  31.0 2.6 copy.52
  36.0 11.7 %cholesky.838 = f32[128,128]{1,0:T(8,128)S(1)} custom-call(f32[128,128]{1,0:T(8,128)S(1)} %cholesky.958), custom_call_target="Cholesky" | custom-call | tf_op jit(solution)/shard_map/jit(cholesky)/cholesky | solution.py:20
  47.8 9.8 custom-call.57
  60.3 11.7 %cholesky.857 = f32[128,128]{1,0:T(8,128)S(1)} custom-call(f32[128,128]{1,0:T(8,128)S(1)} %cholesky.962), custom_call_target="Cholesky" | custom-call | tf_op jit(solution)/shard_map/jit(cholesky)/cholesky | solution.py:20
  72.0 10.0 custom-call.58
  83.5 11.7 %cholesky.878 = f32[128,128]{1,0:T(8,128)S(1)} custom-call(f32[128,128]{1,0:T(8,128)S(1)} %cholesky.967), custom_call_target="Cholesky" | custom-call | tf_op jit(solution)/shard_map/jit(cholesky)/cholesky | solution.py:20
  95.9 9.8 custom-call.59
  107.2 11.7 %cholesky.895 = f32[128,128]{1,0:T(8,128)S(1)} custom-call(f32[128,128]{1,0:T(8,128)S(1)} %convolution_subtract_fusion.30), custom_call_target="Cholesky" | custom-call | tf_op jit(solution)/shard_map/jit(cholesky)/cholesky | solution.py:20
  124.2 11.2 %while.13 = (s32[]{:T(128)}, f32[512,512]{1,0:T(8,128)}, s32[4,2]{0,1:T(2,128)S(1)}, f32[4,128,128]{2,1,0:T(8,128)S(1)}, s32[]{:T(128)}) while((s32[]{:T(128)}, f32[512,512]{1,0:T(8,128)}, s32[4,2]{0,1:T(2,128)S(1)}, f32[4,128,128]{2,1,0:T(8,128)S(1)}, s32[]{:T(128)}) %tuple.218), condition=%wide.while_cond.clone.2, body=%wide.while_body.clone.2.sunk | while | flops 2 | bytes 131189 | solution.py:21
  135.4 39.3 %custom-call.60 = f32[4,128,128]{1,2,0:T(8,128)S(1)} custom-call(f32[4,128,128]{2,1,0:T(8,128)S(1)} %get-tuple-element.166), custom_call_target="InvertDiagBlocksLowerTriangular" | custom-call | tf_op jit(solution)/shard_map/jit(_solve_triangular)/triangular_solve | solution.py:21
  183.3 3.6 all-to-all-start
  186.9 6.0 all-gather.22.cloned.1.call-done
  192.9 3.0 fusion.162
  196.0 4.3 collective-permute-start
  203.4 2.4 collective-permute-done
  207.8 8.4 all-gather.2
  217.3 4.4 collective-permute-start.1
  221.7 7.3 all_gather.73
  231.3 5.1 conditional.7
  236.4 2.3 pad_maximum_fusion.18
  238.7 3.6 all-to-all-start.1
  242.3 14.1 %all-to-all-done.1 = f32[2,512,256]{2,1,0:T(8,128)S(1)} async-done(((f32[2,512,256]{2,1,0:T(8,128)}), f32[2,512,256]{2,1,0:T(8,128)S(1)}, u32[]{:S(2)}, u32[]{:S(2)}) %all-to-all-start.1) | async-done | bytes 1048608 | tf_op jit(solution)/shard_map/all_to_all | solution.py:95
  256.5 152.6 %all-gather.24.cloned.1.call-done = f32[512,512]{1,0:T(8,128)} async-done(((f32[512,256]{1,0:T(8,128)}), f32[512,512]{1,0:T(8,128)}) %all-gather.24.cloned.1.call-update) | async-done | bytes 1048592 | tf_op jit(solution)/shard_map/all_gather | solution.py:97
  409.4 17.5 %collective-permute-start.3 = (f32[256,256]{0,1:T(8,128)S(1)}, f32[256,256]{0,1:T(8,128)S(1)}, u32[]{:S(2)}, u32[]{:S(2)}) collective-permute-start(f32[256,256]{0,1:T(8,128)S(1)} %copy.61), channel_id=1, source_target_pairs={{0,4},{4,8},{8,12},{12,16},{16,20},{20,24},{24,28},{1,5},{5,9},{9,... | collective-permute-start | bytes 786440 | tf_op jit(solution)/shard_map/ppermute | solution.py:12
  428.2 9.3 collective-permute-done.3
  437.6 7.4 all-gather.4
  446.5 5.0 collective-permute-start.5
  451.6 2.4 collective-permute-done.4
  454.0 7.0 all_gather.78
  461.0 2.3 all_gather.79
  463.3 5.0 conditional.9
  468.4 2.3 pad_maximum_fusion.19
  470.7 3.6 all-to-all-start.2
  474.3 14.1 %all-to-all-done.2 = f32[2,512,256]{2,1,0:T(8,128)S(1)} async-done(((f32[2,512,256]{2,1,0:T(8,128)}), f32[2,512,256]{2,1,0:T(8,128)S(1)}, u32[]{:S(2)}, u32[]{:S(2)}) %all-to-all-start.2) | async-done | bytes 1048608 | tf_op jit(solution)/shard_map/all_to_all | solution.py:95
  488.4 159.4 %all-gather.26.cloned.1.call-done = f32[512,512]{1,0:T(8,128)} async-done(((f32[512,256]{1,0:T(8,128)}), f32[512,512]{1,0:T(8,128)}) %all-gather.26.cloned.1.call-update) | async-done | bytes 1048592 | tf_op jit(solution)/shard_map/all_gather | solution.py:97
  648.2 18.6 %collective-permute-start.7 = (f32[256,256]{0,1:T(8,128)S(1)}, f32[256,256]{0,1:T(8,128)S(1)}, u32[]{:S(2)}, u32[]{:S(2)}) collective-permute-start(f32[256,256]{0,1:T(8,128)S(1)} %copy.65), channel_id=1, source_target_pairs={{0,8},{4,12},{8,16},{12,20},{16,24},{20,28},{1,9},{5,13},{9,17},{1... | collective-permute-start | bytes 786440 | tf_op jit(solution)/shard_map/ppermute | solution.py:12
  668.1 3.7 collective-permute-done.7
  671.8 4.1 collective-permute-done.6
  676.7 7.1 all-gather.6
  685.4 4.6 collective-permute-start.9
  689.9 2.4 collective-permute-done.8
  692.4 7.0 all_gather.83
  701.7 5.3 conditional.11
  707.1 2.3 pad_maximum_fusion.20
  709.4 3.6 all-to-all-start.3
  713.0 14.1 %all-to-all-done.3 = f32[2,512,256]{2,1,0:T(8,128)S(1)} async-done(((f32[2,512,256]{2,1,0:T(8,128)}), f32[2,512,256]{2,1,0:T(8,128)S(1)}, u32[]{:S(2)}, u32[]{:S(2)}) %all-to-all-start.3) | async-done | bytes 1048608 | tf_op jit(solution)/shard_map/all_to_all | solution.py:95
  727.1 150.0 %all-gather.28.cloned.1.call-done = f32[512,512]{1,0:T(8,128)} async-done(((f32[512,256]{1,0:T(8,128)}), f32[512,512]{1,0:T(8,128)}) %all-gather.28.cloned.1.call-update) | async-done | bytes 1048592 | tf_op jit(solution)/shard_map/all_gather | solution.py:97
  877.5 20.1 %collective-permute-start.11 = (f32[256,256]{0,1:T(8,128)S(1)}, f32[256,256]{0,1:T(8,128)S(1)}, u32[]{:S(2)}, u32[]{:S(2)}) collective-permute-start(f32[256,256]{0,1:T(8,128)S(1)} %copy.69), channel_id=1, source_target_pairs={{0,16},{4,20},{8,24},{12,28},{1,17},{5,21},{9,25},{13,29},{2,18},{... | collective-permute-start | bytes 786440 | tf_op jit(solution)/shard_map/ppermute | solution.py:12
  898.8 3.7 collective-permute-done.11
  902.5 10.6 collective-permute-done.10
  913.2 7.1 all-gather.8
  922.0 7.8 collective-permute-done.12
  931.9 136.4 %conditional.13 = (f32[128]{0:T(128)S(1)}) conditional(s32[]{:T(128)} %convert_element_type.34, () %tuple.76, (f32[1,512,512]{1,2,0:T(8,128)}, s32[]{:T(128)}) %tuple.256), branch_computations={%region_23.26_spmd, %region_24.28_spmd} | conditional | flops 656916992 | bytes 27548512 | solution.py:145
  935.0 11.7 %cholesky.766 = f32[128,128]{1,0:T(8,128)S(1)} custom-call(f32[128,128]{1,0:T(8,128)S(1)} %cholesky.919), custom_call_target="Cholesky" | custom-call | tf_op jit(solution)/shard_map/cond/branch_1_fun/jit(cholesky)/cholesky | solution.py:20
  946.8 9.8 custom-call.54
  957.4 11.7 %cholesky.785 = f32[128,128]{1,0:T(8,128)S(1)} custom-call(f32[128,128]{1,0:T(8,128)S(1)} %cholesky.923), custom_call_target="Cholesky" | custom-call | tf_op jit(solution)/shard_map/cond/branch_1_fun/jit(cholesky)/cholesky | solution.py:20
  971.1 10.0 custom-call.55
  981.8 11.7 %cholesky.806 = f32[128,128]{1,0:T(8,128)S(1)} custom-call(f32[128,128]{1,0:T(8,128)S(1)} %cholesky.928), custom_call_target="Cholesky" | custom-call | tf_op jit(solution)/shard_map/cond/branch_1_fun/jit(cholesky)/cholesky | solution.py:20
  994.8 9.8 custom-call.56
  1005.2 11.7 %cholesky.823 = f32[128,128]{1,0:T(8,128)S(1)} custom-call(f32[128,128]{1,0:T(8,128)S(1)} %convolution_subtract_fusion.11), custom_call_target="Cholesky" | custom-call | tf_op jit(solution)/shard_map/cond/branch_1_fun/jit(cholesky)/cholesky | solution.py:20
  1018.5 8.1 while.12
  1026.6 39.3 %custom-call.26 = f32[4,128,128]{1,2,0:T(8,128)S(1)} custom-call(f32[4,128,128]{2,1,0:T(8,128)S(1)} %get-tuple-element.144), custom_call_target="InvertDiagBlocksLowerTriangular" | custom-call | tf_op jit(solution)/shard_map/cond/branch_1_fun/jit(_solve_triangular)/triangular_solve | solution.py:21
  (239 shorter events, 82.1 us)
Async XLA Ops:
  7.2 12.1 %copy-start.36 = (f32[2,256,256]{2,1,0:T(8,128)S(1)}, f32[2,256,256]{2,1,0:T(8,128)}, u32[]{:S(2)}) copy-start(f32[2,256,256]{2,1,0:T(8,128)} %param.20) | copy-start | bytes 1572868
  7.2 23.8 %all-gather.20.cloned.1.call-start = ((), (), s32[]{:S(2)}) async-start(), calls=%async_computation.4 | async-start | bytes 1572864 | tf_op jit(solution)/shard_map/all_gather | solution.py:42
  9.2 10.3 copy-start.19
  19.2 173.7 %all-gather.22.cloned.1.call-start = ((), (), s32[]{:S(2)}) async-start(), calls=%async_computation.5 | async-start | bytes 1572864 | tf_op jit(solution)/shard_map/all_gather | solution.py:97
  21.8 9.2 copy-start.13
  31.0 2.7 copy-start.6
  35.1 1.0 copy-start.12
  178.9 2.5 copy-start
  183.3 18.8 %all-to-all-start = ((f32[2,512,256]{2,1,0:T(8,128)}), f32[2,512,256]{2,1,0:T(8,128)S(1)}, u32[]{:S(2)}, u32[]{:S(2)}) async-start(f32[2,512,256]{2,1,0:T(8,128)} %pad_maximum_fusion.17), calls=%async_computation | async-start | bytes 2097152 | tf_op jit(solution)/shard_map/all_to_all | solution.py:95
  186.9 44.4 %all-gather.30.cloned.1.call-start = ((), (), s32[]{:S(2)}) async-start(), calls=%async_computation.9 | async-start | bytes 1572864 | tf_op jit(solution)/shard_map/all_gather | solution.py:42
  196.0 9.8 collective-permute-start
  207.8 8.5 copy-start.17
  216.3 192.8 %all-gather.24.cloned.1.call-start = ((), (), s32[]{:S(2)}) async-start(), calls=%async_computation.6 | async-start | bytes 1572864 | tf_op jit(solution)/shard_map/all_gather | solution.py:97
  217.3 14.0 %copy-start.15 = (f32[256,256]{0,1:T(8,128)}, f32[256,256]{0,1:T(8,128)S(1)}, u32[]{:S(2)}) copy-start(f32[256,256]{0,1:T(8,128)S(1)} %convolution_negate_fusion.3) | copy-start | bytes 786436
  217.3 11.8 %collective-permute-start.1 = (f32[256,256]{0,1:T(8,128)S(1)}, f32[256,256]{0,1:T(8,128)S(1)}, u32[]{:S(2)}, u32[]{:S(2)}) collective-permute-start(f32[256,256]{0,1:T(8,128)S(1)} %convolution_negate_fusion.3), channel_id=1, source_target_pairs={{0,4},{4,8},{8,12},{12,16},{16,20},{20,24},{24,28},{1,5},{5,9},{9,... | collective-permute-start | bytes 786440 | tf_op jit(solution)/shard_map/ppermute | solution.py:12
  238.7 17.7 %all-to-all-start.1 = ((f32[2,512,256]{2,1,0:T(8,128)}), f32[2,512,256]{2,1,0:T(8,128)S(1)}, u32[]{:S(2)}, u32[]{:S(2)}) async-start(f32[2,512,256]{2,1,0:T(8,128)} %pad_maximum_fusion.18), calls=%async_computation.1 | async-start | bytes 2097152 | tf_op jit(solution)/shard_map/all_to_all | solution.py:95
  242.3 221.0 %all-gather.32.cloned.1.call-start = ((), (), s32[]{:S(2)}) async-start(), calls=%async_computation.10 | async-start | bytes 1572864 | tf_op jit(solution)/shard_map/all_gather | solution.py:42
  409.0 28.5 %copy-start.18 = (f32[256,256]{0,1:T(8,128)S(1)}, f32[256,256]{0,1:T(8,128)}, u32[]{:S(2)}) copy-start(f32[256,256]{0,1:T(8,128)} %copy-done.17) | copy-start | bytes 786436
  409.4 44.6 %copy-start.16 = (f32[256,256]{0,1:T(8,128)S(1)}, f32[256,256]{0,1:T(8,128)}, u32[]{:S(2)}) copy-start(f32[256,256]{0,1:T(8,128)} %copy-done.15) | copy-start | bytes 786436
  409.4 28.1 %collective-permute-start.3 = (f32[256,256]{0,1:T(8,128)S(1)}, f32[256,256]{0,1:T(8,128)S(1)}, u32[]{:S(2)}, u32[]{:S(2)}) collective-permute-start(f32[256,256]{0,1:T(8,128)S(1)} %copy.61), channel_id=1, source_target_pairs={{0,4},{4,8},{8,12},{12,16},{16,20},{20,24},{24,28},{1,5},{5,9},{9,... | collective-permute-start | bytes 786440 | tf_op jit(solution)/shard_map/ppermute | solution.py:12
  426.9 10.6 collective-permute-start.2
  437.6 14.0 %copy-start.25 = (f32[256,256]{0,1:T(8,128)}, f32[256,256]{0,1:T(8,128)S(1)}, u32[]{:S(2)}) copy-start(f32[256,256]{0,1:T(8,128)S(1)} %subtract_subtract_fusion.2) | copy-start | bytes 786436
  445.0 202.8 %all-gather.26.cloned.1.call-start = ((), (), s32[]{:S(2)}) async-start(), calls=%async_computation.7 | async-start | bytes 1572864 | tf_op jit(solution)/shard_map/all_gather | solution.py:97
  445.2 8.7 collective-permute-start.4
  446.5 14.5 %collective-permute-start.5 = (f32[256,256]{1,0:T(8,128)S(1)}, f32[256,256]{1,0:T(8,128)S(1)}, u32[]{:S(2)}, u32[]{:S(2)}) collective-permute-start(f32[256,256]{1,0:T(8,128)S(1)} %get-tuple-element.115), channel_id=1, source_target_pairs={{0,4},{4,8},{8,12},{12,16},{16,20},{20,24},{24,28},{1,5},{5,9},{9,... | collective-permute-start | bytes 786440 | tf_op jit(solution)/shard_map/ppermute | solution.py:12
  454.0 9.4 copy-start.23
  468.3 2.4 copy-start.32
  470.7 17.7 %all-to-all-start.2 = ((f32[2,512,256]{2,1,0:T(8,128)}), f32[2,512,256]{2,1,0:T(8,128)S(1)}, u32[]{:S(2)}, u32[]{:S(2)}) async-start(f32[2,512,256]{2,1,0:T(8,128)} %pad_maximum_fusion.19), calls=%async_computation.2 | async-start | bytes 2097152 | tf_op jit(solution)/shard_map/all_to_all | solution.py:95
  474.3 227.4 %all-gather.34.cloned.1.call-start = ((), (), s32[]{:S(2)}) async-start(), calls=%async_computation.11 | async-start | bytes 1572864 | tf_op jit(solution)/shard_map/all_gather | solution.py:42
  647.9 28.1 %copy-start.26 = (f32[256,256]{0,1:T(8,128)S(1)}, f32[256,256]{0,1:T(8,128)}, u32[]{:S(2)}) copy-start(f32[256,256]{0,1:T(8,128)} %copy-done.25) | copy-start | bytes 786436
  648.2 35.7 %copy-start.33 = (f32[256,256]{1,0:T(8,128)S(1)}, f32[256,256]{1,0:T(8,128)}, u32[]{:S(2)}) copy-start(f32[256,256]{1,0:T(8,128)} %copy-done.32) | copy-start | bytes 786436
  648.2 44.1 %copy-start.24 = (f32[256,256]{0,1:T(8,128)S(1)}, f32[256,256]{0,1:T(8,128)}, u32[]{:S(2)}) copy-start(f32[256,256]{0,1:T(8,128)} %copy-done.23) | copy-start | bytes 786436
  648.2 23.6 %collective-permute-start.7 = (f32[256,256]{0,1:T(8,128)S(1)}, f32[256,256]{0,1:T(8,128)S(1)}, u32[]{:S(2)}, u32[]{:S(2)}) collective-permute-start(f32[256,256]{0,1:T(8,128)S(1)} %copy.65), channel_id=1, source_target_pairs={{0,8},{4,12},{8,16},{12,20},{16,24},{20,28},{1,9},{5,13},{9,17},{1... | collective-permute-start | bytes 786440 | tf_op jit(solution)/shard_map/ppermute | solution.py:12
  666.8 9.1 collective-permute-start.6
  676.0 0.7 copy-start.21
  683.8 193.3 %all-gather.28.cloned.1.call-start = ((), (), s32[]{:S(2)}) async-start(), calls=%async_computation.8 | async-start | bytes 1572864 | tf_op jit(solution)/shard_map/all_gather | solution.py:97
  684.0 8.3 collective-permute-start.8
  685.4 14.0 %collective-permute-start.9 = (f32[256,256]{1,0:T(8,128)S(1)}, f32[256,256]{1,0:T(8,128)S(1)}, u32[]{:S(2)}, u32[]{:S(2)}) collective-permute-start(f32[256,256]{1,0:T(8,128)S(1)} %copy-done.33), channel_id=1, source_target_pairs={{0,8},{4,12},{8,16},{12,20},{16,24},{20,28},{1,9},{5,13},{9,17},{1... | collective-permute-start | bytes 786440 | tf_op jit(solution)/shard_map/ppermute | solution.py:12
  692.3 9.4 copy-start.27
  707.0 2.4 copy-start.34
  709.4 17.7 %all-to-all-start.3 = ((f32[2,512,256]{2,1,0:T(8,128)}), f32[2,512,256]{2,1,0:T(8,128)S(1)}, u32[]{:S(2)}, u32[]{:S(2)}) async-start(f32[2,512,256]{2,1,0:T(8,128)} %pad_maximum_fusion.20), calls=%async_computation.3 | async-start | bytes 2097152 | tf_op jit(solution)/shard_map/all_to_all | solution.py:95
  713.0 218.9 %all-gather.36.cloned.1.call-start = ((), (), s32[]{:S(2)}) async-start(), calls=%async_computation.12 | async-start | bytes 1572864 | tf_op jit(solution)/shard_map/all_gather | solution.py:42
  877.1 36.1 %copy-start.22 = (f32[256,256]{0,1:T(8,128)S(1)}, f32[256,256]{0,1:T(8,128)}, u32[]{:S(2)}) copy-start(f32[256,256]{0,1:T(8,128)} %copy-done.21) | copy-start | bytes 786436
  877.4 43.0 %copy-start.35 = (f32[256,256]{1,0:T(8,128)S(1)}, f32[256,256]{1,0:T(8,128)}, u32[]{:S(2)}) copy-start(f32[256,256]{1,0:T(8,128)} %copy-done.34) | copy-start | bytes 786436
  877.5 44.4 %copy-start.1 = (f32[128,640]{1,0:T(8,128)S(1)}, f32[128,640]{1,0:T(8,128)}, u32[]{:S(2)}) copy-start(f32[128,640]{1,0:T(8,128)} %copy-done) | copy-start | bytes 983044
  877.5 25.1 %collective-permute-start.11 = (f32[256,256]{0,1:T(8,128)S(1)}, f32[256,256]{0,1:T(8,128)S(1)}, u32[]{:S(2)}, u32[]{:S(2)}) collective-permute-start(f32[256,256]{0,1:T(8,128)S(1)} %copy.69), channel_id=1, source_target_pairs={{0,16},{4,20},{8,24},{12,28},{1,17},{5,21},{9,25},{13,29},{2,18},{... | collective-permute-start | bytes 786440 | tf_op jit(solution)/shard_map/ppermute | solution.py:12
  897.5 15.6 %collective-permute-start.10 = (f32[256,256]{0,1:T(8,128)S(1)}, f32[256,256]{0,1:T(8,128)S(1)}, u32[]{:S(2)}, u32[]{:S(2)}) collective-permute-start(f32[256,256]{0,1:T(8,128)S(1)} %copy.68), channel_id=1, source_target_pairs={{16,0},{20,4},{24,8},{28,12},{17,1},{21,5},{25,9},{29,13},{18,2},{... | collective-permute-start | bytes 786440 | tf_op jit(solution)/shard_map/ppermute | solution.py:12
  920.4 9.4 copy-start.28
  920.4 9.4 copy-start.14
  920.6 9.2 collective-permute-start.12
  922.0 8.8 copy-start.20
  932.0 1.8 copy-start.5
  934.0 1.0 copy-start.10
  935.0 21.7 %copy-start.11 = (f32[512,512]{1,0:T(8,128)S(1)}, f32[512,512]{1,0:T(8,128)}, u32[]{:S(2)}) copy-start(f32[512,512]{1,0:T(8,128)} %copy-done.10) | copy-start | bytes 3145732 | tf_op jit(solution)/shard_map/cond
Sparse Core Ops, SparseCore 0:
  19.4 10.5 all-gather.19
  182.4 10.5 all-gather.21
  216.4 11.2 all-gather.29
  236.5 172.4 all-gather.23
  445.1 10.5 all-gather.31
  468.5 179.3 all-gather.25
  684.0 7.7 all-gather.33
  707.2 169.8 all-gather.27
  920.5 5.4 all-gather.35
